TPU v7x, 32 devices: a whole 2x2x4 slice. The times are simulated.
32 devices in a mesh: row: 2 (over x), col: 16 (over z, y, core).
Axes of the slice: x: 2, y: 2, z: 4, core: 2. Of those that a mesh axis runs over, the one named last changes fastest.
Arguments:
- adjacency: int32 [2048, 64], P('row', 'col'), may hold values from -2147483648 to 2147483647, as said below
- tile_mask: int32 [16, 16], P('row', 'col'), may hold values from 0 to 1, as said below
- thresholds: int32 [3], replicated, may hold values from 30 to 61
Outputs:
- truss_support: float32 [2048, 2048], P('row', 'col')
- edge_counts: int32 [3], replicated
Inputs may be any that keep to these rules, and one draw needn't show every extreme that they name: The graph of adjacency is symmetric with an empty diagonal: bit b of word w of row i equals the bit for row 32 w + b and column i. `tile_mask`: Symmetric.
All inputs are finite; a program needn't handle non-finite values.
Results may differ from a plain program's by a relative error of at most 0.0003.
Values may be sent and summed in bfloat16 or wider, within the bound.
A program may use at most 64 MiB of HBM per device.

v0:
```python
import functools

import jax
import jax.numpy as jnp
from jax import lax
from jax.experimental import pallas as pl
from jax.experimental.pallas import tpu as pltpu
from jax.sharding import PartitionSpec as P

TILE = 128
ITERS = 3
BITS = 32
MESH = pl.DeviceIdType.MESH


def unpack_words(load_row, words, width, dtype):
    bit = lax.broadcasted_iota(jnp.int32, (BITS, width), 0)
    parts = []
    for w in range(words):
        row = jnp.broadcast_to(load_row(w), (BITS, width))
        parts.append(jnp.bitwise_and(jnp.right_shift(row, bit), 1).astype(jnp.float32).astype(dtype))
    return parts


def kernel(
    n_row, n_col, adj_ref, mask_ref, thr_ref, out_ref, count_ref,
    gath, cross, lhs, rhs, acc, live, tally, tallies,
    send_a, recv_a, send_f, recv_f, send_x, recv_x, send_c, recv_c, turned, out_sem,
):
    words, rows = adj_ref.shape
    cols = words * BITS
    pairs = n_col // 2
    n_dev = n_row * n_col
    my_row, my_col = lax.axis_index("row"), lax.axis_index("col")
    my_pair, my_core = my_col // 2, lax.rem(my_col, 2)
    me = my_row * n_col + my_col
    tiles_here = rows // TILE

    def device(flat):
        return (flat // n_col, lax.rem(flat, n_col))

    barrier = pltpu.get_barrier_semaphore()

    def greet(d, c):
        pl.semaphore_signal(
            barrier, inc=1, device_id=device(lax.rem(me + d, n_dev)), device_id_type=MESH
        )
        return c

    lax.fori_loop(1, n_dev, greet, 0)

    def keep_own(t, w, value):
        gath[t, my_col, w : w + 1, :] = value
        cross[t, my_row, w : w + 1, :] = value

    for w in range(words):
        keep_own(
            0, w,
            jnp.concatenate(
                [adj_ref[w : w + 1, i * TILE : (i + 1) * TILE] * mask_ref[0, i] for i in range(tiles_here)],
                axis=1,
            ),
        )
    tally[...] = jnp.zeros_like(tally)
    lane = lax.broadcasted_iota(jnp.int32, (1, TILE), 1)
    pl.semaphore_wait(barrier, n_dev - 1)

    def direct(t, d):
        return pltpu.make_async_remote_copy(
            src_ref=gath.at[t, my_col], dst_ref=gath.at[t, my_col],
            send_sem=send_a.at[t, d], recv_sem=recv_a.at[t, d],
            device_id=(my_row, shifted(my_pair, d, 1) * 2 + my_core), device_id_type=MESH,
        )

    def relayed(d):
        return d % 2 == 0 or d == 1

    def forward(t, d):
        slot = shifted(my_pair, d, -1) * 2 + my_core if relayed(d) else my_col
        pair = my_pair if relayed(d) else shifted(my_pair, d, 1)
        return pltpu.make_async_remote_copy(
            src_ref=gath.at[t, slot], dst_ref=gath.at[t, slot],
            send_sem=send_f.at[t, d], recv_sem=recv_f.at[t, d],
            device_id=(my_row, pair * 2 + 1 - my_core), device_id_type=MESH,
        )

    def across(t, d):
        return pltpu.make_async_remote_copy(
            src_ref=gath.at[t, my_col], dst_ref=cross.at[t, my_row],
            send_sem=send_x.at[t, d], recv_sem=recv_x.at[t, d],
            device_id=(lax.rem(my_row + d, n_row), my_col), device_id_type=MESH,
        )

    order = sorted(
        range(1, pairs), key=lambda d: (min(d // 2, pairs // 2 - d // 2) + d % 2, d % 2)
    )

    def shifted(pair, d, sign):
        slow = lax.rem(pair // 2 + sign * (d // 2) + pairs // 2, pairs // 2)
        return slow * 2 + lax.rem(pair + d, 2)

    def multiply(t, d):
        pair = shifted(my_pair, d, -1)
        for core in range(2):
            slot = pair * 2 + core
            parts = unpack_words(lambda w: gath[t, slot, w : w + 1, :], words, rows, jnp.bfloat16)
            for w in range(words):
                rhs[core * cols + w * BITS : core * cols + (w + 1) * BITS, :] = parts[w]
        return jnp.dot(lhs[pair], rhs[...], preferred_element_type=jnp.float32)

    for t in range(ITERS):
        threshold = thr_ref[t].astype(jnp.float32)
        for d in range(1, n_row):
            across(t, d).start()
        forward(t, 0).start()

        for d in order:
            direct(t, d).start()
            if not relayed(d):
                forward(t, d).start()

        parts = unpack_words(lambda w: gath[t, my_col, w : w + 1, :], words, rows, jnp.float32)
        for w in range(words):
            live[w * BITS : (w + 1) * BITS, :] = parts[w]
        for d in range(1, n_row):
            across(t, d).wait_recv()
        wide = 2 * cols
        for r in range(n_row):
            parts = unpack_words(lambda w: cross[t, r, w : w + 1, :], words, rows, jnp.bfloat16)
            for w in range(words):
                for q in range(rows // wide):
                    lhs[r * (rows // wide) + q, w * BITS : (w + 1) * BITS, :] = parts[w][:, q * wide : (q + 1) * wide]

        def arrive(d):
            direct(t, d).wait_recv()
            if relayed(d):
                forward(t, d).start()

        arrive(order[0])
        forward(t, 0).wait_recv()
        acc[...] = multiply(t, 0)
        for d, later in zip(order, order[1:] + [None]):
            if later is not None:
                arrive(later)
            forward(t, d).wait_recv()
            acc[...] += multiply(t, d)

        support = acc[...] * live[...]
        kept = jnp.where(support >= threshold, live[...], 0.0)
        if t < ITERS - 1:
            bit = jnp.left_shift(1, lax.broadcasted_iota(jnp.int32, (BITS, rows), 0))
            for w in range(words):
                own = jnp.where(kept[w * BITS : (w + 1) * BITS, :] > 0.0, bit, 0)
                keep_own(t + 1, w, jnp.sum(own, axis=0, keepdims=True))
        per_row = jnp.sum(kept, axis=0, keepdims=True)
        lanes = per_row[:, :TILE]
        for i in range(1, tiles_here):
            lanes = lanes + per_row[:, i * TILE : (i + 1) * TILE]
        here = jnp.sum(lanes.astype(jnp.int32), axis=1, keepdims=True)
        tally[...] = jnp.where(lane == t, here, tally[...])

    def leave(i):
        tile = pl.ds(i * TILE, TILE)
        return pltpu.make_async_copy(turned.at[tile], out_ref.at[tile], out_sem.at[i])

    def count(d):
        return pltpu.make_async_remote_copy(
            src_ref=tally, dst_ref=tallies.at[me],
            send_sem=send_c.at[d], recv_sem=recv_c.at[d],
            device_id=device(lax.rem(me + d, n_dev)), device_id_type=MESH,
        )

    def send_count(d, c):
        count(n_dev - d).start()
        return c

    lax.fori_loop(1, n_dev, send_count, 0)
    tallies[me] = tally[...]
    ratio = support * kept / threshold
    for i in range(tiles_here):
        turned[i * TILE : (i + 1) * TILE, :] = ratio[:, i * TILE : (i + 1) * TILE].T
        leave(i).start()

    def finish_count(d, c):
        count(d).wait()
        return c

    for t in range(ITERS):
        for d in range(1, n_row):
            across(t, d).wait_send()
        forward(t, 0).wait_send()

        for d in order:
            direct(t, d).wait_send()
            forward(t, d).wait_send()
    lax.fori_loop(1, n_dev, finish_count, 0)
    for i in range(tiles_here):
        leave(i).wait()
    total = jnp.sum(tallies[...], axis=0)
    for t in range(ITERS):
        count_ref[t] = jnp.sum(jnp.where(lane == t, total, 0))


def local(n_row, n_col, adjacency, tile_mask, thresholds):
    packed = adjacency.T
    words, rows = packed.shape
    cols = words * BITS
    n_dev = n_row * n_col
    pairs = n_col // 2
    dma = pltpu.SemaphoreType.DMA
    return pl.pallas_call(
        functools.partial(kernel, n_row, n_col),
        out_shape=(
            jax.ShapeDtypeStruct((rows, cols), jnp.float32),
            jax.ShapeDtypeStruct((ITERS,), jnp.int32),
        ),
        in_specs=[
            pl.BlockSpec(memory_space=pltpu.VMEM),
            pl.BlockSpec(memory_space=pltpu.SMEM),
            pl.BlockSpec(memory_space=pltpu.SMEM),
        ],
        out_specs=(
            pl.BlockSpec(memory_space=pl.ANY),
            pl.BlockSpec(memory_space=pltpu.SMEM),
        ),
        scratch_shapes=[
            pltpu.VMEM((ITERS, n_col, words, rows), jnp.int32),
            pltpu.VMEM((ITERS, n_row, words, rows), jnp.int32),
            pltpu.VMEM((pairs, cols, 2 * cols), jnp.bfloat16),
            pltpu.VMEM((2 * cols, rows), jnp.bfloat16),
            pltpu.VMEM((cols, rows), jnp.float32),
            pltpu.VMEM((cols, rows), jnp.float32),
            pltpu.VMEM((1, TILE), jnp.int32),
            pltpu.VMEM((n_dev, 1, TILE), jnp.int32),
            dma((ITERS, pairs)), dma((ITERS, pairs)),
            dma((ITERS, pairs)), dma((ITERS, pairs)),
            dma((ITERS, n_row)), dma((ITERS, n_row)),
            dma((n_dev,)), dma((n_dev,)),
            pltpu.VMEM((rows, cols), jnp.float32), dma((rows // TILE,)),
        ],
        compiler_params=pltpu.CompilerParams(collective_id=0, has_side_effects=True),
    )(packed, tile_mask.T, thresholds)


def solution(mesh):
    in_specs = (P("row", "col"), P("row", "col"), P())
    out_specs = (P("row", "col"), P())
    body = functools.partial(local, mesh.shape["row"], mesh.shape["col"])
    return jax.shard_map(body, mesh=mesh, in_specs=in_specs, out_specs=out_specs, check_vma=False)
```

profile of v0, /device:TPU:0, one launch (start us, length us, event | category | flops | bytes accessed | tf_op | source)
XLA Modules:
  0.0 39.9 jit_solution(8426097465611473828)
XLA Ops:
  0.6 36.9 %shard_map.50 = (f32[1024,128]{1,0:T(8,128)}, s32[3]{0:T(128)}) custom-call(s32[4,1024]{1,0:T(4,128)} %bitcast.2, s32[1,8]{1,0:T(1,128)} %bitcast.3, s32[3]{0:T(128)} %thr_ref.1), custom_call_target="tpu_custom_call" | custom-call | tf_op jit(solution)/shard_map/pallas_call | solution.py:211
  37.6 0.0 copy-start
  37.6 1.9 %copy.7 = f32[1024,128]{1,0:T(8,128)} copy(f32[1024,128]{1,0:T(8,128)} %get-tuple-element.4) | data formatting | bytes 1048576
  39.4 0.0 copy-done
  39.4 0.5 %copy.8 = s32[3]{0:T(128)} copy(s32[3]{0:T(128)S(1)} %copy-done) | data formatting | bytes 24
Async XLA Ops:
  37.6 1.9 %copy-start = (s32[3]{0:T(128)S(1)}, s32[3]{0:T(128)}, u32[]{:S(2)}) copy-start(s32[3]{0:T(128)} %get-tuple-element.5) | copy-start | bytes 40
where the time goes:
time: 40.2 us; the launch traced here: 39.9 us
  Pallas kernels  36.9 us (92%)
  local copies, waits for them, and re-layouts  2.38 us (6%)
  between operations  0.65 us (2%)
    pallas_call x1, Pallas kernels, local(): pl.pallas_call(functools.partial(kernel, n_row, n_col), out_shape=(jax.Sh...  36.9 us
    unnamed x4, local copies, waits for them, and re-layouts  2.38 us

commit v1 on v0

v1 whole, which is shorter than its diff:
```python
import functools

import jax
import jax.numpy as jnp
from jax import lax
from jax.experimental import pallas as pl
from jax.experimental.pallas import tpu as pltpu
from jax.sharding import PartitionSpec as P

TILE = 128
ITERS = 3
BITS = 32
MESH = pl.DeviceIdType.MESH


def wrap(i, n):
    return jnp.where(i >= n, i - n, i)


def spread(load_row, words, width):
    bit = lax.broadcasted_iota(jnp.int32, (BITS, width), 0)
    parts = []
    for w in range(words):
        row = jnp.broadcast_to(load_row(w), (BITS, width))
        parts.append(jnp.bitwise_and(jnp.right_shift(row, bit), 1).astype(jnp.float32))
    return parts


def planes(words):
    return [jnp.bitwise_and(jnp.right_shift(words, b), 1).astype(jnp.float32) for b in range(BITS)]


def kernel(
    n_row, n_col, adj_ref, mask_ref, thr_ref, out_ref, count_ref,
    first, cols0, own, gath, cols, lhs, rhs, acc, tally, tallies, turned, landed,
    send_g, recv_g, send_h, recv_h, send_s, recv_s, send_x, recv_x,
    send_c, recv_c, send_o, recv_o, out_sem,
):
    words, rows = adj_ref.shape
    wide = 2 * words * BITS
    half = rows // 2
    pairs = n_col // 2
    n_dev = n_row * n_col
    my_row, my_col = lax.axis_index("row"), lax.axis_index("col")
    my_pair, my_core = my_col // 2, lax.rem(my_col, 2)
    other = 1 - my_core
    tiles_here = rows // TILE
    per_half = half // wide

    def shifted(pair, d, sign):
        slow = lax.rem(pair // 2 + sign * (d // 2) + pairs // 2, pairs // 2)
        return slow * 2 + lax.rem(pair + d, 2)

    def peer(dr, dc):
        return (wrap(my_row + dr, n_row), wrap(my_col + dc, n_col))

    def each_peer(body):
        if n_dev <= 64:
            for d in range(1, n_dev):
                body(d, peer(d // n_col, d % n_col))
        else:
            def step(d, c):
                body(d, peer(d // n_col, lax.rem(d, n_col)))
                return c

            lax.fori_loop(1, n_dev, step, 0)

    barrier = pltpu.get_barrier_semaphore()
    each_peer(
        lambda d, dev: pl.semaphore_signal(barrier, inc=1, device_id=dev, device_id_type=MESH)
    )

    cols0[my_row, my_core] = jnp.concatenate(
        [adj_ref[:, i * TILE : (i + 1) * TILE] * mask_ref[0, i] for i in range(tiles_here)], axis=1
    )
    pl.semaphore_wait(barrier, n_dev - 1)

    def remote(src, dst, send, recv, dev):
        return pltpu.make_async_remote_copy(
            src_ref=src, dst_ref=dst, send_sem=send, recv_sem=recv, device_id=dev, device_id_type=MESH
        )

    def block(t):
        return cols0.at[my_row, my_core] if t == 0 else own.at[t - 1]

    def gather(t, d, h):
        dev = (my_row, shifted(my_pair, d, 1) * 2 + (h if t == 0 else my_core))
        if t == 0:
            return remote(
                cols0.at[my_row, my_core, :, h * half : (h + 1) * half], first.at[my_pair, my_core],
                send_h.at[d, h], recv_h.at[d, my_core], dev,
            )
        return remote(own.at[t - 1], gath.at[t - 1, my_pair], send_g.at[t - 1, d], recv_g.at[t - 1, d], dev)

    def arrived(t, d):
        if t > 0:
            gather(t, d, 0).wait_recv()
        else:
            for c in range(2):
                src = shifted(my_pair, d, -1)
                remote(
                    first.at[src, c], first.at[src, c], send_h.at[d, c], recv_h.at[d, c], (my_row, my_col)
                ).wait_recv()

    def landing(t):
        return cols0.at[my_row, my_core] if t == 0 else cols.at[t - 1, my_row, my_core]

    def sibling(t):
        return remote(block(t), landing(t), send_s.at[t], recv_s.at[t], (my_row, my_pair * 2 + other))

    def across(t, d, c):
        return remote(
            block(t), landing(t), send_x.at[t, d, c], recv_x.at[t, d, my_core],
            (wrap(my_row + d, n_row), my_pair * 2 + c),
        )

    def across_arrived(t, d, c):
        return remote(
            block(t), landing(t), send_x.at[t, d, c], recv_x.at[t, d, c], (my_row, my_col)
        )

    far = lambda d: min(d // 2, pairs // 2 - d // 2) + d % 2
    order = sorted(range(1, pairs), key=lambda d: (far(d), d % 2))

    def multiply(t, group):
        k = 0
        left, total = [], 0
        for d in group:
            src = shifted(my_pair, d, -1)
            if d == 0:
                load = lambda s: own_words(t)[s : s + 1, :]
                if t > 0:
                    load = lambda s: own[t - 1, s : s + 1, :]
            elif t == 0:
                load = lambda s: first[src, s // words, s % words : s % words + 1, :]
            else:
                load = lambda s: gath[t - 1, src, s : s + 1, :]
            for s, part in enumerate(spread(load, 2 * words, half)):
                rhs[d, s * BITS : (s + 1) * BITS, :] = part.astype(jnp.bfloat16)
            left.append((src, d))
        for src, d in left:
            total = total + jnp.dot(lhs[src], rhs[d], preferred_element_type=jnp.float32)
        return total

    def own_words(t):
        if t > 0:
            return own[t - 1]
        rows_of = pl.ds(pl.multiple_of(my_core * half, half), half)
        return jnp.concatenate([cols0[my_row, c, :, rows_of] for c in range(2)], axis=0)

    def build(t, r):
        for h in range(2):
            if t == 0:
                part = jnp.concatenate(
                    [cols0[r, c, :, h * half : (h + 1) * half] for c in range(2)], axis=0
                )
            else:
                part = cols[t - 1, r, h]
            if t < ITERS - 1:
                full = jnp.concatenate(planes(part), axis=0)
            else:
                full = jnp.concatenate(
                    spread(lambda s: cols[t - 1, r, h, s : s + 1, :], 2 * words, half), axis=0
                )
            full = full.astype(jnp.bfloat16)
            for q in range(per_half):
                lhs[(r * 2 + h) * per_half + q] = full[:, q * wide : (q + 1) * wide]

    def lanes(v):
        total = v[:, :TILE]
        for i in range(1, v.shape[1] // TILE):
            total = total + v[:, i * TILE : (i + 1) * TILE]
        return jnp.sum(total, axis=0, keepdims=True)

    for t in range(ITERS):
        threshold = thr_ref[t].astype(jnp.float32)
        for d in range(1, n_row):
            for c in range(2):
                across(t, d, c).start()
        sibling(t).start()
        for d in reversed(order):
            for h in range(2 if t == 0 else 1):
                gather(t, d, h).start()

        sibling(t).wait_recv()
        for d in range(1, n_row):
            for c in range(2):
                across_arrived(t, d, c).wait_recv()
        for r in range(n_row):
            build(t, r)

        groups = [[0]]
        for i in range(0, len(order), 2):
            groups.append(order[i : i + 2])
        for i, group in enumerate(groups):
            for d in group:
                if d:
                    arrived(t, d)
            if i == 0:
                acc[...] = multiply(t, group)
            elif i < len(groups) - 1:
                acc[...] += multiply(t, group)
            else:
                wedges = acc[...] + multiply(t, group)

        held = own_words(t)
        if t < ITERS - 1:
            size = 2 * words
            stay = jnp.zeros_like(held)
            for b in range(BITS):
                bit = jnp.int32(-(2**31) if b == 31 else 2**b)
                stay = stay | jnp.where(wedges[b * size : (b + 1) * size, :] >= threshold, bit, 0)
            held = held & stay
            own[t] = held
            cols[t, my_row, my_core] = held
            tally[t : t + 1, :] = lanes(lax.population_count(held))
        else:
            live = jnp.concatenate(spread(lambda s: held[s : s + 1, :], 2 * words, half), axis=0)
            kept = (live > 0.0) & (wedges >= threshold)
            tally[t : t + 1, :] = lanes(jnp.where(kept, 1.0, 0.0)).astype(jnp.int32)

    def count(d, dev):
        return remote(tally, tallies.at[my_row * n_col + my_col], send_c.at[d], recv_c.at[d], dev)

    each_peer(lambda d, dev: count(d, dev).start())
    tallies[my_row * n_col + my_col] = tally[...]

    ratio = jnp.where(kept, wedges, 0.0) / threshold
    for c in range(2):
        for i in range(half // TILE):
            turned[c, i * TILE : (i + 1) * TILE, :] = ratio[
                c * (wide // 2) : (c + 1) * (wide // 2), i * TILE : (i + 1) * TILE
            ].T
    swap = remote(turned.at[other], landed, send_o, recv_o, (my_row, my_pair * 2 + other))
    swap.start()
    mine = pltpu.make_async_copy(
        turned.at[my_core], out_ref.at[pl.ds(pl.multiple_of(my_core * half, half), half)], out_sem.at[0]
    )
    mine.start()
    swap.wait_recv()
    theirs = pltpu.make_async_copy(
        landed, out_ref.at[pl.ds(pl.multiple_of(other * half, half), half)], out_sem.at[1]
    )
    theirs.start()

    for t in range(ITERS):
        for d in range(1, n_row):
            for c in range(2):
                across(t, d, c).wait_send()
        sibling(t).wait_send()
        for d in order:
            for h in range(2 if t == 0 else 1):
                gather(t, d, h).wait_send()
    swap.wait_send()
    each_peer(lambda d, dev: count(d, dev).wait())
    total = jnp.sum(jnp.sum(tallies[...], axis=0), axis=1, keepdims=True)
    for t in range(ITERS):
        count_ref[t] = total[t, 0]
    mine.wait()
    theirs.wait()


def local(n_row, n_col, adjacency, tile_mask, thresholds):
    packed = adjacency.T
    words, rows = packed.shape
    cols = words * BITS
    half = rows // 2
    n_dev = n_row * n_col
    pairs = n_col // 2
    dma = pltpu.SemaphoreType.DMA
    return pl.pallas_call(
        functools.partial(kernel, n_row, n_col),
        out_shape=(
            jax.ShapeDtypeStruct((rows, cols), jnp.float32),
            jax.ShapeDtypeStruct((ITERS,), jnp.int32),
        ),
        in_specs=[
            pl.BlockSpec(memory_space=pltpu.VMEM),
            pl.BlockSpec(memory_space=pltpu.SMEM),
            pl.BlockSpec(memory_space=pltpu.SMEM),
        ],
        out_specs=(
            pl.BlockSpec(memory_space=pl.ANY),
            pl.BlockSpec(memory_space=pltpu.SMEM),
        ),
        scratch_shapes=[
            pltpu.VMEM((pairs, 2, words, half), jnp.int32),
            pltpu.VMEM((n_row, 2, words, rows), jnp.int32),
            pltpu.VMEM((ITERS - 1, 2 * words, half), jnp.int32),
            pltpu.VMEM((ITERS - 1, pairs, 2 * words, half), jnp.int32),
            pltpu.VMEM((ITERS - 1, n_row, 2, 2 * words, half), jnp.int32),
            pltpu.VMEM((pairs, 2 * cols, 2 * cols), jnp.bfloat16),
            pltpu.VMEM((pairs, 2 * cols, half), jnp.bfloat16),
            pltpu.VMEM((2 * cols, half), jnp.float32),
            pltpu.VMEM((ITERS, TILE), jnp.int32),
            pltpu.VMEM((n_dev, ITERS, TILE), jnp.int32),
            pltpu.VMEM((2, half, cols), jnp.float32),
            pltpu.VMEM((half, cols), jnp.float32),
            dma((ITERS - 1, pairs)), dma((ITERS - 1, pairs)),
            dma((pairs, 2)), dma((pairs, 2)),
            dma((ITERS,)), dma((ITERS,)),
            dma((ITERS, n_row, 2)), dma((ITERS, n_row, 2)),
            dma((n_dev,)), dma((n_dev,)),
            dma, dma, dma((2,)),
        ],
        compiler_params=pltpu.CompilerParams(collective_id=0, has_side_effects=True),
    )(packed, tile_mask.T, thresholds)


def solution(mesh):
    in_specs = (P("row", "col"), P("row", "col"), P())
    out_specs = (P("row", "col"), P())
    body = functools.partial(local, mesh.shape["row"], mesh.shape["col"])
    return jax.shard_map(body, mesh=mesh, in_specs=in_specs, out_specs=out_specs, check_vma=False)
```

time: 40.2 us -> 34.2 us (0.85)
  Pallas kernels: 36.9 us -> 30.9 us
    pallas_call x1, Pallas kernels: 36.9 us -> 30.9 us  [local(): pl.pallas_call(functools.partial(kernel, n_row, n_col), out_shape=(jax.Sh...]
where the time goes in v1:
time: 34.2 us; the launch traced here: 34 us
  Pallas kernels  30.9 us (90%)
  local copies, waits for them, and re-layouts  2.38 us (7%)
  between operations  0.65 us (2%)
    pallas_call x1, Pallas kernels, local(): pl.pallas_call(functools.partial(kernel, n_row, n_col), out_shape=(jax.Sh...  30.9 us
    unnamed x4, local copies, waits for them, and re-layouts  2.38 us

profile of v1, /device:TPU:0, one launch (start us, length us, event | category | flops | bytes accessed | tf_op | source)
XLA Modules:
  0.0 34.0 jit_solution(3974951805011486174)
XLA Ops:
  0.6 30.9 %shard_map.50 = (f32[1024,128]{1,0:T(8,128)}, s32[3]{0:T(128)}) custom-call(s32[4,1024]{1,0:T(4,128)} %bitcast.2, s32[1,8]{1,0:T(1,128)} %bitcast.3, s32[3]{0:T(128)} %thr_ref.1), custom_call_target="tpu_custom_call" | custom-call | tf_op jit(solution)/shard_map/pallas_call | solution.py:271
  31.6 0.0 copy-start
  31.6 1.9 %copy.7 = f32[1024,128]{1,0:T(8,128)} copy(f32[1024,128]{1,0:T(8,128)} %get-tuple-element.4) | data formatting | bytes 1048576
  33.4 0.0 copy-done
  33.5 0.5 %copy.8 = s32[3]{0:T(128)} copy(s32[3]{0:T(128)S(1)} %copy-done) | data formatting | bytes 24
Async XLA Ops:
  31.6 1.9 %copy-start = (s32[3]{0:T(128)S(1)}, s32[3]{0:T(128)}, u32[]{:S(2)}) copy-start(s32[3]{0:T(128)} %get-tuple-element.5) | copy-start | bytes 40

commit v2 on v1

--- a/solution.py
+++ b/solution.py
@@ -31,10 +31,10 @@
 
 
 def kernel(
-    n_row, n_col, adj_ref, mask_ref, thr_ref, out_ref, count_ref,
+    n_row, n_col, adj_hbm, mask_hbm, thr_hbm, out_ref, count_ref, adj_ref, mask_ref, thr_ref,
     first, cols0, own, gath, cols, lhs, rhs, acc, tally, tallies, turned, landed,
     send_g, recv_g, send_h, recv_h, send_s, recv_s, send_x, recv_x,
-    send_c, recv_c, send_o, recv_o, out_sem,
+    send_c, recv_c, send_o, recv_o, load_sem,
 ):
     words, rows = adj_ref.shape
     wide = 2 * words * BITS
@@ -47,9 +47,13 @@
     tiles_here = rows // TILE
     per_half = half // wide
 
+    depth = (pairs - 1).bit_length()
+    swaps = pairs == 2**depth
+
     def shifted(pair, d, sign):
-        slow = lax.rem(pair // 2 + sign * (d // 2) + pairs // 2, pairs // 2)
-        return slow * 2 + lax.rem(pair + d, 2)
+        if swaps:
+            return sum(lax.rem(pair // 2**i + d // 2**i % 2, 2) * 2**i for i in range(depth))
+        return lax.rem(pair + sign * d + pairs, pairs)
 
     def peer(dr, dc):
         return (wrap(my_row + dr, n_row), wrap(my_col + dc, n_col))
@@ -65,15 +69,25 @@
 
             lax.fori_loop(1, n_dev, step, 0)
 
+    loads = [
+        pltpu.make_async_copy(src, dst, load_sem.at[i])
+        for i, (src, dst) in enumerate(((adj_hbm, adj_ref), (mask_hbm, mask_ref), (thr_hbm, thr_ref)))
+    ]
+    for load in loads:
+        load.start()
+
     barrier = pltpu.get_barrier_semaphore()
-    each_peer(
-        lambda d, dev: pl.semaphore_signal(barrier, inc=1, device_id=dev, device_id_type=MESH)
-    )
+    near = [peer(0, d) for d in range(1, n_col)]
+    near += [(wrap(my_row + d, n_row), my_pair * 2 + c) for d in range(1, n_row) for c in range(2)]
+    for dev in near:
+        pl.semaphore_signal(barrier, inc=1, device_id=dev, device_id_type=MESH)
+    for load in loads:
+        load.wait()
 
     cols0[my_row, my_core] = jnp.concatenate(
         [adj_ref[:, i * TILE : (i + 1) * TILE] * mask_ref[0, i] for i in range(tiles_here)], axis=1
     )
-    pl.semaphore_wait(barrier, n_dev - 1)
+    pl.semaphore_wait(barrier, len(near))
 
     def remote(src, dst, send, recv, dev):
         return pltpu.make_async_remote_copy(
@@ -119,8 +133,7 @@
             block(t), landing(t), send_x.at[t, d, c], recv_x.at[t, d, c], (my_row, my_col)
         )
 
-    far = lambda d: min(d // 2, pairs // 2 - d // 2) + d % 2
-    order = sorted(range(1, pairs), key=lambda d: (far(d), d % 2))
+    order = sorted(range(1, pairs), key=lambda d: d // 2 + d % 2)
 
     def multiply(t, group):
         k = 0
@@ -233,16 +246,9 @@
             ].T
     swap = remote(turned.at[other], landed, send_o, recv_o, (my_row, my_pair * 2 + other))
     swap.start()
-    mine = pltpu.make_async_copy(
-        turned.at[my_core], out_ref.at[pl.ds(pl.multiple_of(my_core * half, half), half)], out_sem.at[0]
-    )
-    mine.start()
+    out_ref[pl.ds(pl.multiple_of(my_core * half, half), half), :] = turned[my_core]
     swap.wait_recv()
-    theirs = pltpu.make_async_copy(
-        landed, out_ref.at[pl.ds(pl.multiple_of(other * half, half), half)], out_sem.at[1]
-    )
-    theirs.start()
-
+    out_ref[pl.ds(pl.multiple_of(other * half, half), half), :] = landed[...]
     for t in range(ITERS):
         for d in range(1, n_row):
             for c in range(2):
@@ -256,8 +262,6 @@
     total = jnp.sum(jnp.sum(tallies[...], axis=0), axis=1, keepdims=True)
     for t in range(ITERS):
         count_ref[t] = total[t, 0]
-    mine.wait()
-    theirs.wait()
 
 
 def local(n_row, n_col, adjacency, tile_mask, thresholds):
@@ -271,19 +275,22 @@
     return pl.pallas_call(
         functools.partial(kernel, n_row, n_col),
         out_shape=(
-            jax.ShapeDtypeStruct((rows, cols), jnp.float32),
-            jax.ShapeDtypeStruct((ITERS,), jnp.int32),
+            pltpu.VMEM((rows, cols), jnp.float32),
+            pltpu.SMEM((ITERS,), jnp.int32),
         ),
         in_specs=[
-            pl.BlockSpec(memory_space=pltpu.VMEM),
-            pl.BlockSpec(memory_space=pltpu.SMEM),
-            pl.BlockSpec(memory_space=pltpu.SMEM),
+            pl.BlockSpec(memory_space=pl.ANY),
+            pl.BlockSpec(memory_space=pl.ANY),
+            pl.BlockSpec(memory_space=pl.ANY),
         ],
         out_specs=(
-            pl.BlockSpec(memory_space=pl.ANY),
+            pl.BlockSpec(memory_space=pltpu.VMEM),
             pl.BlockSpec(memory_space=pltpu.SMEM),
         ),
         scratch_shapes=[
+            pltpu.VMEM((words, rows), jnp.int32),
+            pltpu.SMEM((1, rows // TILE), jnp.int32),
+            pltpu.SMEM((ITERS,), jnp.int32),
             pltpu.VMEM((pairs, 2, words, half), jnp.int32),
             pltpu.VMEM((n_row, 2, words, rows), jnp.int32),
             pltpu.VMEM((ITERS - 1, 2 * words, half), jnp.int32),
@@ -301,7 +308,7 @@
             dma((ITERS,)), dma((ITERS,)),
             dma((ITERS, n_row, 2)), dma((ITERS, n_row, 2)),
             dma((n_dev,)), dma((n_dev,)),
-            dma, dma, dma((2,)),
+            dma, dma, dma((3,)),
         ],
         compiler_params=pltpu.CompilerParams(collective_id=0, has_side_effects=True),
     )(packed, tile_mask.T, thresholds)

time: 34.2 us -> 30.3 us (0.89)
  Pallas kernels: 30.9 us -> 28.1 us
  local copies, waits for them, and re-layouts: 2.38 us -> 1.31 us
    pallas_call x1, Pallas kernels: 30.9 us -> 28.1 us  [local(): pl.pallas_call(functools.partial(kernel, n_row, n_col), out_shape=(pltpu....]
    unnamed x4 -> x2, local copies, waits for them, and re-layouts: 2.38 us -> 1.31 us
where the time goes in v2:
time: 30.3 us; the launch traced here: 30.1 us
  Pallas kernels  28.1 us (93%)
  local copies, waits for them, and re-layouts  1.31 us (4%)
  between operations  0.64 us (2%)
    pallas_call x1, Pallas kernels, local(): pl.pallas_call(functools.partial(kernel, n_row, n_col), out_shape=(pltpu....  28.1 us
    unnamed x2, local copies, waits for them, and re-layouts  1.31 us

profile of v2, /device:TPU:0, one launch (start us, length us, event | category | flops | bytes accessed | tf_op | source)
XLA Modules:
  0.0 30.1 jit_solution(8338548534169524511)
XLA Ops:
  0.6 28.1 %shard_map.50 = (f32[1024,128]{1,0:T(8,128)S(1)}, s32[3]{0:T(128)S(4)}) custom-call(s32[4,1024]{1,0:T(4,128)} %bitcast.2, s32[1,8]{1,0:T(1,128)} %bitcast.3, s32[3]{0:T(128)} %thr_hbm.1), custom_call_target="tpu_custom_call" | custom-call | tf_op jit(solution)/shard_map/pallas_call | solution.py:275
  28.7 0.8 %copy.7 = f32[1024,128]{1,0:T(8,128)} copy(f32[1024,128]{1,0:T(8,128)S(1)} %get-tuple-element.2) | data formatting | bytes 1048576
  29.5 0.5 %copy.8 = s32[3]{0:T(128)} copy(s32[3]{0:T(128)S(4)} %get-tuple-element.3) | data formatting | bytes 24
